TPU v7x, 32 devices: a whole 2x2x4 slice. The times are simulated.
32 devices in a mesh: mkt: 8 (over z, x), grp: 4 (over y, core).
Axes of the slice: x: 2, y: 2, z: 4, core: 2. Of those that a mesh axis runs over, the one named last changes fastest.
Arguments:
- mean_utility: float32 [512, 64], P(('mkt', 'grp')), may hold values from -5 to -1
- market_share: float32 [512, 64], P(('mkt', 'grp')), may hold values from 0.001 to 0.02
- product_traits: float32 [512, 64, 5], P(('mkt', 'grp')), may hold values from -1 to 1
- taste_draws: float32 [512, 5, 1024], P(('mkt', 'grp')), may hold values from -4 to 4
- taste_scale: float32 [5], replicated, may hold values from 0.3 to 1
- type_weight: float32 [512, 1024], P(('mkt', 'grp')), may hold values from 0.1 to 1
- market_size: float32 [512], P(('mkt', 'grp')), may hold values from 0.05 to 3
- product_firm: int32 [512, 64], P(('mkt', 'grp')), may hold values from 0 to 511, all different within a row
- firm_order: int32 [512], replicated, may hold values from 0 to 511, each once
- loyalty: float32 [512, 1024], P(('mkt', 'grp')), may hold values from -1 to 1
- firm_share: float32 [512, 1024], replicated, may hold values from 2e-05 to 0.15
Outputs:
- utility_out: float32 [512, 64], P(('mkt', 'grp'))
- loyalty_out: float32 [512, 1024], P(('mkt', 'grp'))
Inputs may be any that keep to these rules, and one draw needn't show every extreme that they name: `product_firm`: in each market the 64 products belong to 64 different firms, and every firm sells in some market. `firm_order`: each firm appears once.
All inputs are finite; a program needn't handle non-finite values.
Results may differ from a plain program's by a relative error of at most 0.0001.
Values sent between devices are 32-bit elements; how exact they have to be, the bound alone decides.
A program may use at most 64 MiB of HBM per device.

v0:
```python
import jax
import jax.numpy as jnp
from jax import lax
from jax.sharding import PartitionSpec as P

ITERS = 3


clip_target = 0.5
norm_eps = 1e-06


def inverse_order(firm_order):
    count = firm_order.shape[0]
    return jnp.zeros((count,), jnp.int32).at[firm_order].set(jnp.arange(count, dtype=jnp.int32))


def market_terms(mean_now, taste, type_weight, mass, row_ids, table):
    expu = jnp.exp(mean_now[:, :, None] + taste + jnp.take(table, row_ids, axis=0))
    choice_prob = expu / (1.0 + jnp.sum(expu, axis=1, keepdims=True))
    weighted_sum = jnp.einsum(
        "mjr,mr->mj", choice_prob, type_weight, precision=lax.Precision.HIGHEST
    )
    weighted = choice_prob * mass[:, None, :]
    firm_count = table.shape[0]
    onehot = (
        jnp.arange(firm_count, dtype=jnp.int32)[:, None] == row_ids.reshape(-1)[None, :]
    ).astype(jnp.float32)
    partial_value = jnp.dot(
        onehot,
        weighted.reshape(-1, weighted.shape[2]),
        precision=lax.Precision.HIGHEST,
        preferred_element_type=jnp.float32,
    )
    return (weighted_sum, partial_value)


def local(
    mean_utility,
    market_share,
    product_traits,
    taste_draws,
    taste_scale,
    type_weight,
    market_size,
    product_firm,
    firm_order,
    loyalty,
    firm_share,
):
    firm_count = firm_share.shape[0]
    draw_count = firm_share.shape[1]
    owned_count = loyalty.shape[0]
    devices = lax.axis_size(("mkt", "grp"))
    inverse = inverse_order(firm_order)
    owner_rows = jnp.take(inverse, product_firm, axis=0)
    owned = loyalty
    my_firms = lax.dynamic_slice_in_dim(
        firm_order, lax.axis_index(("mkt", "grp")) * owned_count, owned_count
    )
    taste = jnp.einsum(
        "mjk,mkr->mjr", product_traits * taste_scale, taste_draws, precision=lax.Precision.HIGHEST
    )
    weight_total = jnp.sum(type_weight, axis=1)
    mass = market_size[:, None] * type_weight
    type_mass = lax.psum(jnp.sum(mass, axis=0), ("mkt", "grp"))
    log_observed = jnp.log(market_share)
    mean_now = mean_utility
    my_share = jnp.log(jnp.take(firm_share, my_firms, axis=0))
    for step in range(ITERS):
        table = lax.all_gather(owned, ("mkt", "grp"), axis=0, tiled=True)
        weighted_sum, by_owner = market_terms(mean_now, taste, type_weight, mass, owner_rows, table)
        predicted = weighted_sum / weight_total[:, None]
        blocks = by_owner.reshape(devices, owned_count, draw_count)
        received = lax.all_to_all(blocks, ("mkt", "grp"), split_axis=0, concat_axis=0, tiled=True)
        own_totals = jnp.sum(received, axis=0)
        gap = my_share - jnp.log(own_totals / type_mass[None, :])
        squares = lax.psum(jnp.sum(gap * gap), ("mkt", "grp"))
        clip = jnp.minimum(
            1.0, clip_target / jnp.sqrt(squares / (firm_count * draw_count) + norm_eps)
        )
        owned = owned + clip * gap
        mean_now = mean_now + log_observed - jnp.log(predicted)
    return (mean_now, owned)


def solution(mesh):
    placed = (
        P(("mkt", "grp"), None),
        P(("mkt", "grp"), None),
        P(("mkt", "grp"), None, None),
        P(("mkt", "grp"), None, None),
        P(),
        P(("mkt", "grp"), None),
        P(("mkt", "grp")),
        P(("mkt", "grp"), None),
        P(),
        P(("mkt", "grp"), None),
        P(),
    )
    return jax.shard_map(
        local,
        mesh=mesh,
        in_specs=placed,
        out_specs=(P(("mkt", "grp"), None), P(("mkt", "grp"), None)),
        check_vma=False,
    )
```

profile of v0, /device:TPU:0, one launch (start us, length us, event | category | flops | bytes accessed | tf_op | source)
XLA Modules:
  0.0 555.0 jit_solution(14951167932557971051)
XLA Ops:
  7.2 0.7 all-gather.4.cloned.1.call-update
  7.9 0.7 compare_select_fusion.1
  8.7 0.7 compare_select_fusion.2
  9.4 2.4 scatter_custom_fusion
  11.9 6.9 %gather_fusion = s32[1024]{0:T(1024)S(1)} fusion(s32[512]{0:T(512)S(1)} %scatter_custom_fusion, s32[1024]{0:T(1024)S(1)} %broadcast_clamp_fusion.1), kind=kCustom, calls=%fused_computation.3 | custom fusion | bytes 12288 | tf_op jit(solution)/shard_map/jit(_take)/gather | solution.py:56
  19.1 50.8 %all-gather.4.cloned.1.call-done = f32[512,1024]{1,0:T(8,128)} async-done(((f32[16,1024]{1,0:T(8,128)}), f32[512,1024]{1,0:T(8,128)}) %all-gather.4.cloned.1.call-update) | async-done | bytes 2097168 | tf_op jit(solution)/shard_map/all_gather | solution.py:71
  69.9 8.0 %gather_fusion.2 = f32[1024,1024]{1,0:T(8,128)} fusion(f32[512,1024]{1,0:T(8,128)} %all-gather.4.cloned.1.call-done, s32[1024]{0:T(1024)S(1)} %broadcast_clamp_fusion), kind=kCustom, calls=%fused_computation.clone | custom fusion | bytes 8392704 | tf_op jit(solution)/shard_map/jit(_take)/gather | solution.py:19
  77.9 7.5 %fusion.31 = (f32[16,1024]{1,0:T(8,128)S(1)}, f32[16,64,1024]{2,1,0:T(8,128)S(1)}, f32[16,64,1024]{2,1,0:T(8,128)}) fusion(f32[16,64,1024]{2,1,0:T(8,128)} %bitcast.24, pred[16,64]{1,0:T(8,128)(4,1)S(1)} %get-tuple-element.19, f32[16,64]{1,0:T(8,128)S(1)} %copy-done.11, f32[16,5,1024]{2,0,1:T(8,128)S(1)} %copy-done.4, ...), kind=kOutput, calls=%fused_computation.73 | convolution fusion | flops 67092480 | bytes 13001728 | tf_op jit(solution)/shard_map/mjk,mkr->mjr/dot_general | solution.py:61
  85.4 0.1 fusion.30
  85.6 1.0 broadcast_multiply_fusion.2
  86.5 1.3 copy-done.1
  87.8 5.0 fusion.7
  92.8 3.6 all-to-all-start
  96.5 0.8 compare_and_fusion.1
  97.3 0.6 gather_fusion.1
  97.9 67.7 %psum.28 = f32[1024]{0:T(1024)S(1)} all-reduce(f32[1024]{0:T(1024)S(1)} %get-tuple-element.15), channel_id=1, replica_groups=mesh['mkt'=8,'grp'=4] {'mkt','grp'}, use_global_device_ids=true, to_apply=%region_5.7 | all-reduce | flops 1024 | bytes 8192 | tf_op jit(solution)/shard_map/psum | solution.py:66
  165.5 1.7 reduce_sum.101
  167.2 0.7 multiply_reduce_fusion.2
  167.9 38.4 %psum.29 = f32[]{:T(128)} all-reduce(f32[]{:T(128)} %get-tuple-element.11), channel_id=1, replica_groups=mesh['mkt'=8,'grp'=4] {'mkt','grp'}, use_global_device_ids=true, to_apply=%region_7.9 | all-reduce | flops 1 | bytes 8 | tf_op jit(solution)/shard_map/psum | solution.py:78
  207.0 0.6 multiply_add_fusion.2
  207.7 0.2 all-gather.8.cloned.1.call-start
  208.0 5.5 fusion.9
  213.6 52.0 %all-gather.6.cloned.1.call-done = f32[512,1024]{1,0:T(8,128)} async-done(((f32[16,1024]{1,0:T(8,128)}), f32[512,1024]{1,0:T(8,128)}) %all-gather.6.cloned.1.call-update) | async-done | bytes 2097168 | tf_op jit(solution)/shard_map/all_gather | solution.py:71
  265.6 8.0 %gather_fusion.3 = f32[1024,1024]{1,0:T(8,128)} fusion(f32[512,1024]{1,0:T(8,128)} %all-gather.6.cloned.1.call-done, s32[1024]{0:T(1024)S(1)} %broadcast_clamp_fusion), kind=kCustom, calls=%fused_computation.1.clone | custom fusion | bytes 8392704 | tf_op jit(solution)/shard_map/jit(_take)/gather | solution.py:19
  273.6 4.0 fusion.28
  277.7 1.0 broadcast_multiply_fusion.1
  278.7 1.3 copy-done.2
  280.0 3.7 fusion.5
  283.7 52.0 %all_to_all.15 = f32[32,16,1024]{2,1,0:T(8,128)} all-to-all(f32[32,16,1024]{2,1,0:T(8,128)S(1)} %fusion.5), channel_id=1, replica_groups=mesh['mkt'=8,'grp'=4] {'mkt','grp'}, dimensions={0} | all-to-all | bytes 4194304 | tf_op jit(solution)/shard_map/all_to_all | solution.py:75
  335.8 1.7 reduce_sum.105
  337.5 0.7 multiply_reduce_fusion.1
  338.2 38.9 %psum.30 = f32[]{:T(128)} all-reduce(f32[]{:T(128)} %get-tuple-element.7), channel_id=1, replica_groups=mesh['mkt'=8,'grp'=4] {'mkt','grp'}, use_global_device_ids=true, to_apply=%region_11.13 | all-reduce | flops 1 | bytes 8 | tf_op jit(solution)/shard_map/psum | solution.py:78
  377.8 0.6 multiply_add_fusion.1
  378.5 5.5 fusion.10
  384.1 50.7 %all-gather.8.cloned.1.call-done = f32[512,1024]{1,0:T(8,128)} async-done(((f32[16,1024]{1,0:T(8,128)}), f32[512,1024]{1,0:T(8,128)}) %all-gather.8.cloned.1.call-update) | async-done | bytes 2097168 | tf_op jit(solution)/shard_map/all_gather | solution.py:71
  434.8 8.0 %gather_fusion.4 = f32[1024,1024]{1,0:T(8,128)} fusion(f32[512,1024]{1,0:T(8,128)} %all-gather.8.cloned.1.call-done, s32[1024]{0:T(1024)S(1)} %broadcast_clamp_fusion), kind=kCustom, calls=%fused_computation.2.clone | custom fusion | bytes 8392704 | tf_op jit(solution)/shard_map/jit(_take)/gather | solution.py:19
  442.8 4.1 fusion.26
  446.9 1.0 broadcast_multiply_fusion
  447.9 1.3 copy-done.3
  449.2 5.0 fusion.3
  454.2 3.6 all-to-all-start.2
  457.8 5.5 fusion.11
  463.4 0.7 log_subtract_fusion.3
  464.1 42.4 %all-to-all-done.2 = f32[32,16,1024]{2,1,0:T(8,128)} async-done(((f32[32,16,1024]{2,1,0:T(8,128)}), f32[32,16,1024]{2,1,0:T(8,128)}, u32[]{:S(2)}, u32[]{:S(2)}) %all-to-all-start.2) | async-done | bytes 2097184 | tf_op jit(solution)/shard_map/all_to_all | solution.py:75
  506.5 1.7 reduce_sum.108
  508.2 0.8 multiply_reduce_fusion
  509.0 38.3 %psum.31 = f32[]{:T(128)} all-reduce(f32[]{:T(128)} %get-tuple-element.3), channel_id=1, replica_groups=mesh['mkt'=8,'grp'=4] {'mkt','grp'}, use_global_device_ids=true, to_apply=%region_15.17 | all-reduce | flops 1 | bytes 8 | tf_op jit(solution)/shard_map/psum | solution.py:78
  547.9 0.6 multiply_add_fusion
  (48 shorter events, 0.8 us)
Async XLA Ops:
  7.2 90.1 %copy-start = (f32[512,1024]{1,0:T(8,128)S(1)}, f32[512,1024]{1,0:T(8,128)}, u32[]{:S(2)}) copy-start(f32[512,1024]{1,0:T(8,128)} %param.23) | copy-start | bytes 6291460
  7.2 62.7 %all-gather.4.cloned.1.call-start = ((), (), s32[]{:S(2)}) async-start(), calls=%async_computation.3 | async-start | bytes 2162688 | tf_op jit(solution)/shard_map/all_gather | solution.py:71
  11.8 7.0 %copy-start.12 = (s32[16,64]{1,0:T(8,128)S(1)}, s32[16,64]{1,0:T(8,128)}, u32[]{:S(2)}) copy-start(s32[16,64]{1,0:T(8,128)} %param.20) | copy-start | bytes 12292
  11.8 7.1 %copy-start.10 = (f32[16,64,5]{1,0,2:T(8,128)S(1)}, f32[16,64,5]{1,0,2:T(8,128)}, u32[]{:S(2)}) copy-start(f32[16,64,5]{1,0,2:T(8,128)} %param.15) | copy-start | bytes 61444
  11.9 7.1 %copy-start.13 = (f32[5]{0:T(128)S(1)}, f32[5]{0:T(128)}, u32[]{:S(2)}) copy-start(f32[5]{0:T(128)} %param.17) | copy-start | bytes 64
  19.1 58.8 %copy-start.4 = (f32[16,5,1024]{2,0,1:T(8,128)S(1)}, f32[16,5,1024]{2,0,1:T(8,128)}, u32[]{:S(2)}) copy-start(f32[16,5,1024]{2,0,1:T(8,128)} %param.16) | copy-start | bytes 983044
  19.1 58.8 %copy-start.11 = (f32[16,64]{1,0:T(8,128)S(1)}, f32[16,64]{1,0:T(8,128)}, u32[]{:S(2)}) copy-start(f32[16,64]{1,0:T(8,128)} %param.13) | copy-start | bytes 12292
  77.9 7.5 %copy-start.9 = (f32[16,1024]{1,0:T(8,128)S(1)}, f32[16,1024]{1,0:T(8,128)}, u32[]{:S(2)}) copy-start(f32[16,1024]{1,0:T(8,128)} %param.18) | copy-start | bytes 196612
  77.9 7.5 %copy-start.14 = (f32[16]{0:T(128)S(1)}, f32[16]{0:T(128)}, u32[]{:S(2)}) copy-start(f32[16]{0:T(128)} %param.19) | copy-start | bytes 196
  85.4 2.4 copy-start.1
  92.8 114.2 %copy-start.7 = (f32[16,1024]{1,0:T(8,128)S(1)}, f32[16,1024]{1,0:T(8,128)}, u32[]{:S(2)}) copy-start(f32[16,1024]{1,0:T(8,128)} %param.22) | copy-start | bytes 196612
  92.8 72.7 %all-to-all-start = ((f32[32,16,1024]{2,1,0:T(8,128)}), f32[32,16,1024]{2,1,0:T(8,128)}, u32[]{:S(2)}, u32[]{:S(2)}) async-start(f32[32,16,1024]{2,1,0:T(8,128)} %fusion.7), calls=%async_computation | async-start | bytes 4194304 | tf_op jit(solution)/shard_map/all_to_all | solution.py:75
  96.4 169.2 %all-gather.6.cloned.1.call-start = ((), (), s32[]{:S(2)}) async-start(), calls=%async_computation.4 | async-start | bytes 2162688 | tf_op jit(solution)/shard_map/all_gather | solution.py:71
  207.7 227.1 %all-gather.8.cloned.1.call-start = ((), (), s32[]{:S(2)}) async-start(), calls=%async_computation.5 | async-start | bytes 2162688 | tf_op jit(solution)/shard_map/all_gather | solution.py:71
  207.9 5.5 copy-start.8
  277.7 2.3 copy-start.2
  283.7 94.1 %copy-start.6 = (f32[16,1024]{1,0:T(8,128)S(1)}, f32[16,1024]{1,0:T(8,128)}, u32[]{:S(2)}) copy-start(f32[16,1024]{1,0:T(8,128)} %multiply_add_fusion.2) | copy-start | bytes 196612
  446.9 2.3 copy-start.3
  454.2 52.3 %all-to-all-start.2 = ((f32[32,16,1024]{2,1,0:T(8,128)}), f32[32,16,1024]{2,1,0:T(8,128)}, u32[]{:S(2)}, u32[]{:S(2)}) async-start(f32[32,16,1024]{2,1,0:T(8,128)} %fusion.3), calls=%async_computation.2 | async-start | bytes 4194304 | tf_op jit(solution)/shard_map/all_to_all | solution.py:75
  457.8 90.0 %copy-start.5 = (f32[16,1024]{1,0:T(8,128)S(1)}, f32[16,1024]{1,0:T(8,128)}, u32[]{:S(2)}) copy-start(f32[16,1024]{1,0:T(8,128)} %multiply_add_fusion.1) | copy-start | bytes 196612
Sparse Core Ops, SparseCore 0:
  10.8 58.9 all-gather.3
  207.8 57.7 all-gather.5
  378.6 56.1 all-gather.7
where the time goes:
time: 557 us; the launch traced here: 555 us
  blocking collectives  235 us (42%)
  waiting for transfers between devices  197 us (35%)
  local copies, waits for them, and re-layouts  38.1 us (7%)
  matrix products  37.9 us (7%)
  other arithmetic  23.5 us (4%)
  between operations  16 us (3%)
  starting transfers between devices  7.5 us (1%)
    all_gather x3, waiting for transfers between devices, local(): table = lax.all_gather(owned, ('mkt', 'grp'), axis=0, tiled=True)  154 us
    psum x3, blocking collectives, local(): squares = lax.psum(jnp.sum(gap * gap), ('mkt', 'grp'))  116 us
    psum x1, blocking collectives, local(): type_mass = lax.psum(jnp.sum(mass, axis=0), ('mkt', 'grp'))  67.7 us
    all_to_all x1, blocking collectives, local(): lax.all_to_all(blocks, ('mkt', 'grp'), split_axis=0, concat_axis=0, tiled...  52 us
    all_to_all x2, waiting for transfers between devices, local(): lax.all_to_all(blocks, ('mkt', 'grp'), split_axis=0, concat_axis=0, tiled...  42.4 us
    gather x3, local copies, waits for them, and re-layouts, market_terms(): jnp.take(table, row_ids, axis=0)  24 us
    dot_general x3, matrix products, market_terms(): jnp.einsum('mjr,mr->mj', choice_prob, type_weight, precision=lax.Precisio...  16.6 us
    dot_general x3, matrix products, market_terms(): jnp.dot(onehot, weighted.reshape(-1, weighted.shape[2]), precision=lax.Pr...  13.8 us
  transfers between devices with their start and end apart: 5, of which 4 were waited for; matrix products, arithmetic and copies ran while one was open for 5% of the time, Pallas kernels for 0%

commit v1 on v0

v1 whole, which is shorter than its diff:
```python
import functools
import math

import jax
import jax.numpy as jnp
from jax import lax
from jax.experimental import pallas as pl
from jax.experimental.pallas import tpu as pltpu
from jax.sharding import PartitionSpec as P

ITERS = 3
LANES = 128
MESH = pl.DeviceIdType.MESH

clip_target = 0.5
norm_eps = 1e-06


def columns(row):
    return jnp.broadcast_to(row, (LANES, LANES)).T


def split_hi_lo(x):
    hi = x.astype(jnp.bfloat16)
    lo = (x - hi.astype(jnp.float32)).astype(jnp.bfloat16)
    return hi, lo


def kernel(
    dims,
    wide_ref, info_ref, loy_ref, base_ref, mean0_ref, order_ref, share_ref,
    mean_out, loy_out,
    wide, info, loy, means, tbl, tq, tmass, tm_own,
    one_hot, one_hot_t, taste, order_col, share_v, weighted, table_hl, acc,
    sums, sums_in, totals, totals_in, gap, squares, squares_in, old, old_in, last, last_in,
    copy_sem, wide_s, info_s, loy_s, mean_s, tq_s, tm_s, sums_s, totals_s, gap_s, old_s, last_s, sq_s,
):
    mkt, grp, rb, groups, n_m, J, K, firms, owned, R = dims
    n = mkt * grp
    rows = n_m * J
    tiles = rows // LANES
    qr = firms // groups
    a = lax.axis_index("mkt")
    b = lax.axis_index("grp")
    ao, ai = a // rb, a % rb
    q_me = ao * grp + b
    me = a * grp + b

    def type_peer(d):
        p = (ai + d) % rb
        return p, (ao * rb + p, b)

    def market_peer(d):
        q = (q_me + d) % groups
        return q, ((q // grp) * rb + ai, q % grp)

    pending = []

    def send(src, dst, sems, mine, theirs, device):
        copy = pltpu.make_async_remote_copy(
            src_ref=src, dst_ref=dst.at[mine], send_sem=sems.at[0, theirs], recv_sem=sems.at[1, mine],
            device_id=device, device_id_type=MESH,
        )
        copy.start()
        pending.append(copy)

    def arrive(dst, sems, theirs, device):
        pltpu.make_async_remote_copy(
            src_ref=dst.at[theirs], dst_ref=dst.at[theirs], send_sem=sems.at[0, theirs], recv_sem=sems.at[1, theirs],
            device_id=device, device_id_type=MESH,
        ).wait_recv()

    def lanes_of(p):
        return pl.ds(pl.multiple_of(p * LANES, LANES), LANES)

    share_copy = pltpu.make_async_copy(share_ref.at[:, lanes_of(ai)], share_v, copy_sem)
    share_copy.start()

    barrier = pltpu.get_barrier_semaphore()

    @pl.loop(1, n)
    def _(d):
        t = (me + d) % n
        pl.semaphore_signal(barrier, inc=1, device_id=(t // grp, t % grp), device_id_type=MESH)

    pl.semaphore_wait(barrier, n - 1)

    for d in range(1, rb):
        p, device = type_peer(d)
        send(loy_ref.at[:, lanes_of(p)], loy, loy_s, ai, p, device)
    for d in range(1, rb):
        p, device = type_peer(d)
        send(info_ref, info, info_s, ai, p, device)
        send(mean0_ref, means.at[0], mean_s.at[0], ai, p, device)
    for d in range(1, rb):
        p, device = type_peer(d)
        send(wide_ref.at[:, lanes_of(p)], wide, wide_s, ai, p, device)

    wide[ai] = wide_ref[:, lanes_of(ai)]
    info[ai] = info_ref[...]
    loy[ai] = loy_ref[:, lanes_of(ai)]
    means[0, ai] = mean0_ref[...]

    for i in range(firms // LANES):
        order_col[i * LANES:(i + 1) * LANES, :] = columns(order_ref[0:1, i * LANES:(i + 1) * LANES])

    for d in range(1, rb):
        p, device = type_peer(d)
        arrive(loy, loy_s, p, device)
    for p in range(rb):
        tq[p * owned:(p + 1) * owned, :] = loy[p]
    for d in range(1, groups):
        q, device = market_peer(d)
        send(tq, tbl, tq_s, q_me, q, device)
    tbl[q_me] = tq[...]

    share_copy.wait()
    first = pl.multiple_of(q_me * qr, 8)
    mine_col = order_col[pl.ds(first, qr), :]
    number = lax.broadcasted_iota(jnp.int32, (qr, LANES), 1).astype(jnp.float32)
    my_share = jnp.zeros((qr, LANES), jnp.float32)
    for i in range(firms // LANES):
        pick = (mine_col == number + float(i * LANES)).astype(jnp.float32)
        my_share += jnp.dot(
            pick, share_v[i * LANES:(i + 1) * LANES, :],
            precision=lax.Precision.HIGHEST, preferred_element_type=jnp.float32,
        )
    my_share = jnp.log(my_share)

    for d in range(1, rb):
        p, device = type_peer(d)
        arrive(info, info_s, p, device)
        arrive(means.at[0], mean_s.at[0], p, device)
    for d in range(1, rb):
        p, device = type_peer(d)
        arrive(wide, wide_s, p, device)

    tm_own[...] = jnp.zeros_like(tm_own)

    @pl.loop(0, rb)
    def _(p):
        tm_own[...] += jnp.sum(wide[p, n_m * K:, :], axis=0, keepdims=True)

    for d in range(1, groups):
        q, device = market_peer(d)
        send(tm_own, tmass, tm_s, q_me, q, device)
    tmass[q_me] = tm_own[...]

    @pl.loop(0, rb)
    def _(p):
        row = lax.broadcasted_iota(jnp.int32, (n_m * K, rows), 0)
        lane = lax.broadcasted_iota(jnp.int32, (n_m * K, rows), 1)
        traits = jnp.zeros((n_m * K, rows), jnp.float32)
        for k in range(K):
            traits = jnp.where(row - (row // K) * K == k, info[p, k:k + 1, :], traits)
        traits = jnp.where(row // K == lane // J, traits, 0.0)
        taste[p] = lax.dot_general(
            traits, wide[p, :n_m * K, :], (((0,), (0,)), ((), ())),
            precision=lax.Precision.HIGHEST, preferred_element_type=jnp.float32,
        )
        for i in range(tiles):
            firm_row = info[p, K:K + 1, i * LANES:(i + 1) * LANES]
            firm_col = columns(firm_row)
            for f in range(firms // LANES):
                one_hot[p, i * LANES:(i + 1) * LANES, f * LANES:(f + 1) * LANES] = (
                    firm_col == order_ref[0:1, f * LANES:(f + 1) * LANES]
                ).astype(jnp.float32).astype(jnp.bfloat16)
            one_hot_t[p, :, i * LANES:(i + 1) * LANES] = (
                order_col[...] == firm_row
            ).astype(jnp.float32).astype(jnp.bfloat16)

    for d in range(1, groups):
        q, device = market_peer(d)
        arrive(tbl, tq_s, q, device)
        arrive(tmass, tm_s, q, device)
    log_mass = jnp.log(jnp.sum(tmass[...], axis=0))

    block = 2 * LANES
    per_block = block // J

    def contract(it):
        for q in range(groups):
            hi, lo = split_hi_lo(tbl[q])
            table_hl[q * qr:(q + 1) * qr, :LANES] = hi
            table_hl[q * qr:(q + 1) * qr, LANES:] = lo
        acc[...] = jnp.zeros_like(acc)

        @pl.loop(0, rb)
        def _(p):
            mean_rows = means[it, p]
            for h in range(rows // block):
                r0 = h * block
                both = jnp.dot(
                    one_hot[p, r0:r0 + block, :], table_hl[...], preferred_element_type=jnp.float32
                )
                mean_col = jnp.concatenate(
                    [columns(mean_rows[2 * h + i:2 * h + i + 1, :]) for i in range(2)], axis=0
                )
                expu = jnp.exp(both[:, :LANES] + both[:, LANES:] + mean_col + taste[p, r0:r0 + block, :])
                parts = []
                for m in range(per_block):
                    part = expu[m * J:(m + 1) * J, :]
                    mass = wide[p, n_m * K + h * per_block + m:n_m * K + h * per_block + m + 1, :]
                    parts.append(part * (mass / (1.0 + jnp.sum(part, axis=0, keepdims=True))))
                bought = jnp.concatenate(parts, axis=0)
                for i in range(2):
                    sums[it, p, 2 * h + i:2 * h + i + 1, :] = jnp.sum(
                        bought[i * LANES:(i + 1) * LANES, :].T, axis=0, keepdims=True
                    )
                hi, lo = split_hi_lo(bought)
                weighted[r0:r0 + block, :LANES] = hi
                weighted[r0:r0 + block, LANES:] = lo
            acc[...] += jnp.dot(one_hot_t[p], weighted[...], preferred_element_type=jnp.float32)

        for q in range(groups):
            totals[it, q] = acc[q * qr:(q + 1) * qr, :LANES] + acc[q * qr:(q + 1) * qr, LANES:]

    mean_now = mean0_ref[...]
    for it in range(ITERS):
        final = it == ITERS - 1
        if final:
            mine = tbl[q_me]
            for p in range(rb):
                old[p] = mine[p * owned:(p + 1) * owned, :]
            for d in range(1, rb):
                p, device = type_peer(d)
                send(old.at[p], old_in, old_s, ai, p, device)
            old_in[ai] = old[ai]
        contract(it)
        for d in range(1, groups):
            q, device = market_peer(d)
            send(totals.at[it, q], totals_in.at[it], totals_s.at[it], q_me, q, device)
        for d in range(1, rb):
            p, device = type_peer(d)
            send(sums.at[it, p], sums_in.at[it], sums_s.at[it], ai, p, device)
        sums_in[it, ai] = sums[it, ai]
        totals_in[it, q_me] = totals[it, q_me]

        for d in range(1, rb):
            p, device = type_peer(d)
            arrive(sums_in.at[it], sums_s.at[it], p, device)
        mean_now = mean_now + base_ref[...] - jnp.log(jnp.sum(sums_in[it], axis=0))
        if final:
            mean_out[...] = mean_now
        else:
            means[it + 1, ai] = mean_now
            for d in range(1, rb):
                p, device = type_peer(d)
                send(means.at[it + 1, ai], means.at[it + 1], mean_s.at[it + 1], ai, p, device)

        for d in range(1, groups):
            q, device = market_peer(d)
            arrive(totals_in.at[it], totals_s.at[it], q, device)
        gap_mine = my_share - (jnp.log(jnp.sum(totals_in[it], axis=0)) - log_mass)
        squares[it] = jnp.sum(gap_mine * gap_mine, axis=0, keepdims=True)

        @pl.loop(1, n)
        def _(d):
            t = (me + d) % n
            pltpu.make_async_remote_copy(
                src_ref=squares.at[it], dst_ref=squares_in.at[it, d - 1],
                send_sem=sq_s.at[0, it], recv_sem=sq_s.at[1, it],
                device_id=(t // grp, t % grp), device_id_type=MESH,
            ).start()

        if final:
            for p in range(rb):
                last[p] = gap_mine[p * owned:(p + 1) * owned, :]
            for d in range(1, rb):
                p, device = type_peer(d)
                send(last.at[p], last_in, last_s, ai, p, device)
            last_in[ai] = last[ai]
        else:
            gap[it, q_me] = gap_mine
            for d in range(1, groups):
                q, device = market_peer(d)
                send(gap.at[it, q_me], gap.at[it], gap_s.at[it], q_me, q, device)

        pltpu.make_async_copy(squares_in.at[it], squares_in.at[it], sq_s.at[1, it]).wait()
        total = jnp.sum(jnp.sum(squares_in[it], axis=0) + squares[it], axis=1, keepdims=True)
        clip = jnp.minimum(1.0, clip_target / jnp.sqrt(total / (firms * R) + norm_eps))

        if final:
            for d in range(1, rb):
                p, device = type_peer(d)
                arrive(old_in, old_s, p, device)
                arrive(last_in, last_s, p, device)
            for p in range(rb):
                loy_out[:, p * LANES:(p + 1) * LANES] = old_in[p] + clip * last_in[p]
        else:
            for d in range(1, groups):
                q, device = market_peer(d)
                arrive(gap.at[it], gap_s.at[it], q, device)
            for q in range(groups):
                tbl[q] = tbl[q] + clip * gap[it, q]
            for d in range(1, rb):
                p, device = type_peer(d)
                arrive(means.at[it + 1], mean_s.at[it + 1], p, device)

    for it in range(ITERS):
        pltpu.make_async_copy(squares_in.at[it], squares_in.at[it], sq_s.at[0, it]).wait()
    for copy in pending:
        copy.wait_send()


def local(
    mkt, grp,
    mean_utility, market_share, product_traits, taste_draws, taste_scale, type_weight,
    market_size, product_firm, firm_order, loyalty, firm_share,
):
    n_m, J, K = product_traits.shape
    firms, R = firm_share.shape
    owned = loyalty.shape[0]
    rb = R // LANES
    groups = mkt * grp // rb
    rows = n_m * J
    tiles = rows // LANES
    qr = firms // groups

    mass = market_size[:, None] * type_weight
    wide_own = jnp.concatenate([taste_draws.reshape(n_m * K, R), mass], axis=0)
    traits = (product_traits * taste_scale).reshape(rows, K).T
    firm = product_firm.astype(jnp.float32).reshape(1, rows)
    height = -(-(K + 1) // 8) * 8
    info_own = jnp.concatenate([traits, firm, jnp.zeros((height - K - 1, rows), jnp.float32)], axis=0)
    base = jnp.log(market_share) + jnp.log(jnp.sum(mass, axis=1))[:, None]
    order = firm_order.astype(jnp.float32).reshape(mkt // rb, rb, grp, owned)
    order = order.transpose(0, 2, 1, 3).reshape(1, firms)

    f32, bf16 = jnp.float32, jnp.bfloat16
    dma = pltpu.SemaphoreType.DMA
    vmem = pltpu.VMEM
    spec = pl.BlockSpec(memory_space=pltpu.VMEM)
    dims = (mkt, grp, rb, groups, n_m, J, K, firms, owned, R)
    scratch = [
        vmem((rb,) + wide_own.shape[:1] + (LANES,), f32),
        vmem((rb, height, rows), f32),
        vmem((rb, owned, LANES), f32),
        vmem((ITERS, rb, tiles, LANES), f32),
        vmem((groups, qr, LANES), f32),
        vmem((qr, LANES), f32),
        vmem((groups, 1, LANES), f32),
        vmem((1, LANES), f32),
        vmem((rb, rows, firms), bf16),
        vmem((rb, firms, rows), bf16),
        vmem((rb, rows, LANES), f32),
        vmem((firms, LANES), f32),
        vmem((firms, LANES), f32),
        vmem((rows, 2 * LANES), bf16),
        vmem((firms, 2 * LANES), bf16),
        vmem((firms, 2 * LANES), f32),
        vmem((ITERS, rb, tiles, LANES), f32),
        vmem((ITERS, rb, tiles, LANES), f32),
        vmem((ITERS, groups, qr, LANES), f32),
        vmem((ITERS, groups, qr, LANES), f32),
        vmem((ITERS - 1, groups, qr, LANES), f32),
        vmem((ITERS, 1, LANES), f32),
        vmem((ITERS, mkt * grp - 1, 1, LANES), f32),
        vmem((rb, owned, LANES), f32),
        vmem((rb, owned, LANES), f32),
        vmem((rb, owned, LANES), f32),
        vmem((rb, owned, LANES), f32),
        dma,
        dma((2, rb)), dma((2, rb)), dma((2, rb)),
        dma((ITERS, 2, rb)),
        dma((2, groups)), dma((2, groups)),
        dma((ITERS, 2, rb)),
        dma((ITERS, 2, groups)),
        dma((ITERS - 1, 2, groups)),
        dma((2, rb)), dma((2, rb)),
        dma((2, ITERS)),
    ]
    mean_new, loyalty_new = pl.pallas_call(
        functools.partial(kernel, dims),
        out_shape=(
            jax.ShapeDtypeStruct((tiles, LANES), f32),
            jax.ShapeDtypeStruct((owned, R), f32),
        ),
        in_specs=[spec] * 6 + [pl.BlockSpec(memory_space=pl.ANY)],
        out_specs=(spec, spec),
        scratch_shapes=scratch,
        compiler_params=pltpu.CompilerParams(
            collective_id=0, has_side_effects=True, vmem_limit_bytes=60 * 1024 * 1024
        ),
    )(
        wide_own, info_own, loyalty, base.reshape(tiles, LANES),
        mean_utility.reshape(tiles, LANES), order, firm_share,
    )
    return mean_new.reshape(n_m, J), loyalty_new


def solution(mesh):
    both = ("mkt", "grp")
    placed = (
        P(both, None), P(both, None), P(both, None, None), P(both, None, None), P(),
        P(both, None), P(both), P(both, None), P(), P(both, None), P(),
    )
    return jax.shard_map(
        functools.partial(local, mesh.shape["mkt"], mesh.shape["grp"]),
        mesh=mesh,
        in_specs=placed,
        out_specs=(P(both, None), P(both, None)),
        check_vma=False,
    )
```

time: 557 us -> 99.4 us (0.18)
  blocking collectives: 235 us -> 0 us
  waiting for transfers between devices: 197 us -> 0 us
  Pallas kernels: 0 us -> 89.2 us
  matrix products: 37.9 us -> 0 us
  local copies, waits for them, and re-layouts: 38.1 us -> 6.43 us
  other arithmetic: 23.5 us -> 2.67 us
  between operations: 16 us -> 0.71 us
  starting transfers between devices: 7.5 us -> 0 us
    psum x4 -> x0, blocking collectives: 183 us -> none  [the longest x3 116 us: local(): squares = lax.psum(jnp.sum(gap * gap), ('mkt', 'grp'))]
    all_gather x3 -> x0, waiting for transfers between devices: 154 us -> none  [local(): table = lax.all_gather(owned, ('mkt', 'grp'), axis=0, tiled=True)]
    pallas_call x0 -> x1, Pallas kernels: none -> 89.2 us  [local(): pl.pallas_call(functools.partial(kernel, dims), out_shape=(jax.ShapeDtype...]
    all_to_all x1 -> x0, blocking collectives: 52 us -> none  [local(): lax.all_to_all(blocks, ('mkt', 'grp'), split_axis=0, concat_axis=0, tiled...]
    all_to_all x2 -> x0, waiting for transfers between devices: 42.4 us -> none  [local(): lax.all_to_all(blocks, ('mkt', 'grp'), split_axis=0, concat_axis=0, tiled...]
    dot_general x7 -> x0, matrix products: 37.9 us -> none  [the longest x3 16.6 us: market_terms(): jnp.einsum('mjr,mr->mj', choice_prob, type_weight, precision=lax.Precisio...]
    gather x6 -> x0, local copies, waits for them, and re-layouts: 31.6 us -> none  [the longest x3 24 us: market_terms(): jnp.take(table, row_ids, axis=0)]
    reduce_sum x9 -> x1, other arithmetic: 15.5 us -> 1.07 us  [local(): base = jnp.log(market_share) + jnp.log(jnp.sum(mass, axis=1))[:, None]]
  transfers between devices with their start and end apart: 5 -> 0, of which waited for: 4 -> 0; matrix products, arithmetic and copies ran while one was open for 5% -> 0% of each run, Pallas kernels for 0% -> 0%
where the time goes in v1:
time: 99.4 us; the launch traced here: 99.1 us
  Pallas kernels  89.2 us (90%)
  local copies, waits for them, and re-layouts  6.43 us (6%)
  other arithmetic  2.67 us (3%)
    pallas_call x1, Pallas kernels, local(): pl.pallas_call(functools.partial(kernel, dims), out_shape=(jax.ShapeDtype...  89.2 us
    unnamed x14, local copies, waits for them, and re-layouts  2.68 us

profile of v1, /device:TPU:0, one launch (start us, length us, event | category | flops | bytes accessed | tf_op | source)
XLA Modules:
  0.0 99.1 jit_solution(8853203829115646081)
XLA Ops:
  0.6 0.0 copy-start.2
  0.6 0.0 copy-start
  0.7 0.0 copy-start.5
  0.7 0.0 copy-start.3
  0.7 0.0 copy-start.4
  0.7 0.0 copy-start.1
  0.7 1.1 %fusion = (f32[16]{0:T(128)S(1)}, f32[16,1024]{1,0:T(8,128)S(1)}) fusion(f32[16,1024]{1,0:T(8,128)} %param.16, f32[16]{0:T(128)} %param.17), kind=kLoop, calls=%fused_computation.5 | loop fusion | flops 32752 | bytes 131200 | tf_op jit(solution)/shard_map/reduce_sum | solution.py:326
  1.8 1.2 %copy.14 = f32[16,5,1024]{2,1,0:T(8,128)S(1)} copy(f32[16,5,1024]{2,0,1:T(8,128)} %param.14) | data formatting | bytes 655360 | tf_op args[3]
  2.9 0.1 reshape.33
  3.0 0.8 pad_maximum_fusion.wide_ref
  3.8 0.0 copy-done.2
  3.8 0.1 log_add_fusion
  3.9 0.7 reshape.36.base_ref
  4.5 0.0 copy-done
  4.5 0.0 copy-done.5
  4.5 0.1 broadcast_multiply_fusion.1
  4.6 0.1 reshape.34
  4.7 0.0 copy-done.3
  4.7 0.1 reshape.35
  4.8 0.1 pad.2.clone
  4.9 0.7 maximum_maximum_fusion.info_ref
  5.5 0.0 copy-done.4
  5.6 0.1 reshape.38
  5.7 0.7 reshape.39.order_ref
  6.3 0.0 copy-done.1
  6.3 0.7 reshape.37.mean0_ref
  7.0 89.2 %shard_map.122 = (f32[8,128]{1,0:T(8,128)}, f32[16,1024]{1,0:T(8,128)}) custom-call(f32[96,1024]{1,0:T(8,128)} %pad_maximum_fusion.wide_ref, f32[8,1024]{1,0:T(8,128)} %maximum_maximum_fusion.info_ref, f32[16,1024]{1,0:T(8,128)} %loy_ref.1, f32[8,128]{1,0:T(8,128)} %reshape.36.base_ref, f32[8,128]{1,0:T(8,128)} %reshape.37.mean0_ref, ...), custom_call_target="tpu_custom_call" | custom-call | tf_op jit(solution)/shard_map/pallas_call | solution.py:373
  96.2 1.3 %reshape.40 = f32[16,64]{1,0:T(8,128)} reshape(f32[8,128]{1,0:T(8,128)} %get-tuple-element.4) | data formatting | bytes 8192 | tf_op jit(solution)/shard_map/reshape | solution.py:389
  97.6 1.5 %copy.17 = f32[16,1024]{1,0:T(8,128)} copy(f32[16,1024]{1,0:T(8,128)} %get-tuple-element.11) | data formatting | bytes 131072
  (5 shorter events, 0.0 us)
Async XLA Ops:
  0.6 3.2 %copy-start.2 = (f32[16,64]{1,0:T(8,128)S(1)}, f32[16,64]{1,0:T(8,128)}, u32[]{:S(2)}) copy-start(f32[16,64]{1,0:T(8,128)} %param.12) | copy-start | bytes 12292
  0.6 3.9 %copy-start = (f32[16,64,5]{1,0,2:T(8,128)S(1)}, f32[16,64,5]{1,0,2:T(8,128)}, u32[]{:S(2)}) copy-start(f32[16,64,5]{1,0,2:T(8,128)} %param.13) | copy-start | bytes 61444
  0.7 3.9 %copy-start.5 = (f32[5]{0:T(128)S(1)}, f32[5]{0:T(128)}, u32[]{:S(2)}) copy-start(f32[5]{0:T(128)} %param.15) | copy-start | bytes 64
  0.7 4.0 %copy-start.3 = (s32[16,64]{1,0:T(8,128)S(1)}, s32[16,64]{1,0:T(8,128)}, u32[]{:S(2)}) copy-start(s32[16,64]{1,0:T(8,128)} %param.18) | copy-start | bytes 12292
  0.7 4.9 %copy-start.4 = (s32[512]{0:T(512)S(1)}, s32[512]{0:T(512)}, u32[]{:S(2)}) copy-start(s32[512]{0:T(512)} %param.19) | copy-start | bytes 6148
  0.7 5.7 %copy-start.1 = (f32[16,64]{1,0:T(8,128)S(1)}, f32[16,64]{1,0:T(8,128)}, u32[]{:S(2)}) copy-start(f32[16,64]{1,0:T(8,128)} %param.11) | copy-start | bytes 12292

commit v2 on v1

v2 whole, which is shorter than its diff:
```python
import functools
import math

import jax
import jax.numpy as jnp
from jax import lax
from jax.experimental import pallas as pl
from jax.experimental.pallas import tpu as pltpu
from jax.sharding import PartitionSpec as P

ITERS = 3
LANES = 128
MESH = pl.DeviceIdType.MESH

clip_target = 0.5
norm_eps = 1e-06


def columns(row):
    return jnp.broadcast_to(row, (LANES, LANES)).T


def split_hi_lo(x):
    hi = x.astype(jnp.bfloat16)
    lo = (x - hi.astype(jnp.float32)).astype(jnp.bfloat16)
    return hi, lo


def kernel(
    dims,
    size_ref, scale_ref, draws_ref, weight_ref, traits_ref, firm_ref, mean_ref, share_own_ref,
    loy_ref, order_ref, share_ref,
    mean_out, loy_out,
    draws, mass, info, loy, means, tbl, tq, tmass, tm_own,
    mass_own, info_own, lmat, one_hot, one_hot_t, taste, col, order_col, order_row, share_v, weighted, table_hl, acc,
    sums, sums_in, totals, totals_in, gap, squares, squares_in, old, old_in, last, last_in,
    copy_sem, draws_s, mass_s, info_s, loy_s, mean_s, tq_s, tm_s, sums_s, totals_s, gap_s, old_s, last_s, sq_s,
):
    mkt, grp, rb, groups, n_m, J, K, firms, owned, R = dims
    n = mkt * grp
    rows = n_m * J
    tiles = rows // LANES
    pair = LANES // J
    qr = firms // groups
    half = groups // 2
    a = lax.axis_index("mkt")
    b = lax.axis_index("grp")
    ao, ai = a // rb, a % rb
    q_me = ao * grp + b
    me = a * grp + b
    side = q_me // half

    barrier = pltpu.get_barrier_semaphore()

    @pl.loop(1, n)
    def _(d):
        t = (me + d) % n
        pl.semaphore_signal(barrier, inc=1, device_id=(t // grp, t % grp), device_id_type=MESH)

    def type_peer(d):
        p = (ai + d) % rb
        return p, (ao * rb + p, b)

    def market_device(q):
        return ((q // grp) * rb + ai, q % grp)

    def market_peer(d):
        q = (q_me + d) % groups
        return q, market_device(q)

    pending = []

    def send(src, dst, sems, mine, theirs, device):
        copy = pltpu.make_async_remote_copy(
            src_ref=src, dst_ref=dst.at[mine], send_sem=sems.at[0, theirs], recv_sem=sems.at[1, mine],
            device_id=device, device_id_type=MESH,
        )
        copy.start()
        pending.append(copy)

    def arrive(dst, sems, theirs, device):
        pltpu.make_async_remote_copy(
            src_ref=dst.at[theirs], dst_ref=dst.at[theirs], send_sem=sems.at[0, theirs], recv_sem=sems.at[1, theirs],
            device_id=device, device_id_type=MESH,
        ).wait_recv()

    def lanes_of(p):
        return pl.ds(pl.multiple_of(p * LANES, LANES), LANES)

    def pack(x):
        return jnp.concatenate([x[i * tiles:(i + 1) * tiles, :] for i in range(pair)], axis=1)

    share_copy = pltpu.make_async_copy(share_ref.at[:, lanes_of(ai)], share_v, copy_sem)
    share_copy.start()

    for k in range(K):
        info_own[k] = pack(traits_ref[k] * scale_ref[k])
    info_own[K] = pack(firm_ref[...].astype(jnp.float32))
    info_own[K + 1] = pack(mean_ref[...])
    for m in range(n_m):
        mass_own[m:m + 1, :] = weight_ref[m:m + 1, :] * size_ref[m]
    info[ai] = info_own[...]

    pl.semaphore_wait(barrier, n - 1)

    for d in range(1, rb):
        p, device = type_peer(d)
        send(loy_ref.at[:, lanes_of(p)], loy, loy_s, ai, p, device)
    for d in range(1, rb):
        p, device = type_peer(d)
        send(info_own, info, info_s, ai, p, device)
        send(draws_ref.at[:, lanes_of(p)], draws, draws_s, ai, p, device)
        send(mass_own.at[:, lanes_of(p)], mass, mass_s, ai, p, device)

    draws[ai] = draws_ref[:, lanes_of(ai)]
    mass[ai] = mass_own[:, lanes_of(ai)]
    loy[ai] = loy_ref[:, lanes_of(ai)]

    for i in range(firms // LANES):
        col[i * LANES:(i + 1) * LANES, :] = columns(order_ref[i:i + 1, :].astype(jnp.float32))
    for q in range(groups):
        for p in range(rb):
            src = (((q // grp) * rb + p) * grp + q % grp) * owned
            dst = (q * rb + p) * owned
            order_col[dst:dst + owned, :] = col[src:src + owned, :]
    for i in range(firms // LANES):
        order_row[0:1, i * LANES:(i + 1) * LANES] = order_col[i * LANES:(i + 1) * LANES, :].T[0:1, :]

    for d in range(1, rb):
        p, device = type_peer(d)
        arrive(loy, loy_s, p, device)
    for p in range(rb):
        tq[p * owned:(p + 1) * owned, :] = loy[p]
    for d in range(1, groups):
        q, device = market_peer(d)
        send(tq, tbl, tq_s, q_me, q, device)
    tbl[q_me] = tq[...]

    row = lax.broadcasted_iota(jnp.int32, (n_m * K, LANES), 0)
    lane = lax.broadcasted_iota(jnp.int32, (n_m * K, LANES), 1)
    trait_of = row // n_m
    offset = row % n_m - (lane // J) * tiles

    def prepare(p):
        for i in range(tiles):
            traits = jnp.zeros((n_m * K, LANES), jnp.float32)
            for k in range(K):
                traits = jnp.where(trait_of == k, info[p, k, i:i + 1, :], traits)
            lmat[:, i * LANES:(i + 1) * LANES] = jnp.where(offset == i, traits, 0.0)
        taste[p] = lax.dot_general(
            lmat[...], draws[p], (((0,), (0,)), ((), ())),
            precision=lax.Precision.HIGHEST, preferred_element_type=jnp.float32,
        )
        for i in range(tiles):
            firm_row = info[p, K, i:i + 1, :]
            firm_col = columns(firm_row)
            for f in range(firms // LANES):
                one_hot[p, i * LANES:(i + 1) * LANES, f * LANES:(f + 1) * LANES] = (
                    firm_col == order_row[0:1, f * LANES:(f + 1) * LANES]
                ).astype(jnp.float32).astype(jnp.bfloat16)
            one_hot_t[p, :, i * LANES:(i + 1) * LANES] = (
                order_col[...] == firm_row
            ).astype(jnp.float32).astype(jnp.bfloat16)

    prepare(ai)

    share_copy.wait()
    first = pl.multiple_of(q_me * qr, 8)
    mine_col = order_col[pl.ds(first, qr), :]
    number = lax.broadcasted_iota(jnp.int32, (qr, LANES), 1).astype(jnp.float32)
    my_share = jnp.zeros((qr, LANES), jnp.float32)
    for i in range(firms // LANES):
        pick = (mine_col == number + float(i * LANES)).astype(jnp.float32)
        my_share += jnp.dot(
            pick, share_v[i * LANES:(i + 1) * LANES, :],
            precision=lax.Precision.HIGHEST, preferred_element_type=jnp.float32,
        )
    my_share = jnp.log(my_share)

    share_own = share_own_ref[...]
    base = jnp.log(share_own) + jnp.log(jnp.sum(mass_own[...], axis=1, keepdims=True))
    base = pack(base)

    for d in range(1, groups):
        q, device = market_peer(d)
        arrive(tbl, tq_s, q, device)

    def split_table():
        for q in range(groups):
            hi, lo = split_hi_lo(tbl[q])
            table_hl[q * qr:(q + 1) * qr, :LANES] = hi
            table_hl[q * qr:(q + 1) * qr, LANES:] = lo

    per_block = 2
    block = per_block * LANES

    def shares(it, p):
        mean_rows = info[p, K + 1] if it == 0 else means[it - 1, p]
        for h in range(rows // block):
            r0 = h * block
            both = jnp.dot(
                one_hot[p, r0:r0 + block, :], table_hl[...], preferred_element_type=jnp.float32
            )
            mean_col = jnp.concatenate(
                [columns(mean_rows[i:i + 1, :]) for i in range(h * per_block, (h + 1) * per_block)], axis=0
            )
            expu = jnp.exp(both[:, :LANES] + both[:, LANES:] + mean_col + taste[p, r0:r0 + block, :])
            parts = []
            for i in range(per_block):
                for s in range(pair):
                    part = expu[i * LANES + s * J:i * LANES + (s + 1) * J, :]
                    m = s * tiles + h * per_block + i
                    parts.append(
                        part * (mass[p, m:m + 1, :] / (1.0 + jnp.sum(part, axis=0, keepdims=True)))
                    )
            bought = jnp.concatenate(parts, axis=0)
            for i in range(per_block):
                at = h * per_block + i
                sums[it, p, at:at + 1, :] = jnp.sum(
                    bought[i * LANES:(i + 1) * LANES, :].T, axis=0, keepdims=True
                )
            hi, lo = split_hi_lo(bought)
            weighted[p, r0:r0 + block, :LANES] = hi
            weighted[p, r0:r0 + block, LANES:] = lo

    def half_totals(it, which):
        begin = pl.multiple_of(which * (half * qr), 16)
        acc[...] = jnp.zeros_like(acc)

        @pl.loop(0, rb)
        def _(p):
            acc[...] += jnp.dot(
                one_hot_t[p, pl.ds(begin, half * qr), :], weighted[p], preferred_element_type=jnp.float32
            )

        for j in range(half):
            totals[it, which * half + j] = (
                acc[j * qr:(j + 1) * qr, :LANES] + acc[j * qr:(j + 1) * qr, LANES:]
            )

    mean_now = pack(mean_ref[...])
    log_mass = None
    for it in range(ITERS):
        final = it == ITERS - 1
        if final:
            mine = tbl[q_me]
            for p in range(rb):
                old[p] = mine[p * owned:(p + 1) * owned, :]
            for d in range(1, rb):
                p, device = type_peer(d)
                send(old.at[p], old_in, old_s, ai, p, device)
            old_in[ai] = old[ai]
        split_table()
        if it == 0:
            shares(0, ai)

            @pl.loop(1, rb)
            def _(d):
                p, device = type_peer(d)
                arrive(info, info_s, p, device)
                arrive(draws, draws_s, p, device)
                arrive(mass, mass_s, p, device)
                prepare(p)
                shares(0, p)

            tm_own[...] = jnp.zeros_like(tm_own)
            for p in range(rb):
                tm_own[...] += jnp.sum(mass[p], axis=0, keepdims=True)
            for d in range(1, groups):
                q, device = market_peer(d)
                send(tm_own, tmass, tm_s, q_me, q, device)
            tmass[q_me] = tm_own[...]
        else:
            @pl.loop(0, rb)
            def _(p):
                shares(it, p)

        for d in range(1, rb):
            p, device = type_peer(d)
            send(sums.at[it, p], sums_in.at[it], sums_s.at[it], ai, p, device)
        sums_in[it, ai] = sums[it, ai]

        half_totals(it, 1 - side)
        for j in range(half):
            q = (1 - side) * half + (q_me + j) % half
            send(totals.at[it, q], totals_in.at[it], totals_s.at[it], q_me, q, market_device(q))
        half_totals(it, side)
        for j in range(1, half):
            q = side * half + (q_me + j) % half
            send(totals.at[it, q], totals_in.at[it], totals_s.at[it], q_me, q, market_device(q))
        totals_in[it, q_me] = totals[it, q_me]

        for d in range(1, rb):
            p, device = type_peer(d)
            arrive(sums_in.at[it], sums_s.at[it], p, device)
        mean_now = mean_now + base - jnp.log(jnp.sum(sums_in[it], axis=0))
        if final:
            for i in range(pair):
                mean_out[i * tiles:(i + 1) * tiles, :] = mean_now[:, i * J:(i + 1) * J]
        else:
            means[it, ai] = mean_now
            for d in range(1, rb):
                p, device = type_peer(d)
                send(means.at[it, ai], means.at[it], mean_s.at[it], ai, p, device)

        if it == 0:
            for d in range(1, groups):
                q, device = market_peer(d)
                arrive(tmass, tm_s, q, device)
            log_mass = jnp.log(jnp.sum(tmass[...], axis=0))
        for d in range(1, groups):
            q, device = market_peer(d)
            arrive(totals_in.at[it], totals_s.at[it], q, device)
        gap_mine = my_share - (jnp.log(jnp.sum(totals_in[it], axis=0)) - log_mass)
        squares[it] = jnp.sum(gap_mine * gap_mine, axis=0, keepdims=True)

        @pl.loop(1, n)
        def _(d):
            t = (me + d) % n
            pltpu.make_async_remote_copy(
                src_ref=squares.at[it], dst_ref=squares_in.at[it, d - 1],
                send_sem=sq_s.at[0, it], recv_sem=sq_s.at[1, it],
                device_id=(t // grp, t % grp), device_id_type=MESH,
            ).start()

        if final:
            for p in range(rb):
                last[p] = gap_mine[p * owned:(p + 1) * owned, :]
            for d in range(1, rb):
                p, device = type_peer(d)
                send(last.at[p], last_in, last_s, ai, p, device)
            last_in[ai] = last[ai]
        else:
            gap[it, q_me] = gap_mine
            for d in range(1, groups):
                q, device = market_peer(d)
                send(gap.at[it, q_me], gap.at[it], gap_s.at[it], q_me, q, device)

        pltpu.make_async_copy(squares_in.at[it], squares_in.at[it], sq_s.at[1, it]).wait()
        total = jnp.sum(jnp.sum(squares_in[it], axis=0) + squares[it], axis=1, keepdims=True)
        clip = jnp.minimum(1.0, clip_target / jnp.sqrt(total / (firms * R) + norm_eps))

        if final:
            for d in range(1, rb):
                p, device = type_peer(d)
                arrive(old_in, old_s, p, device)
                arrive(last_in, last_s, p, device)
            for p in range(rb):
                loy_out[:, p * LANES:(p + 1) * LANES] = old_in[p] + clip * last_in[p]
        else:
            for d in range(1, groups):
                q, device = market_peer(d)
                arrive(gap.at[it], gap_s.at[it], q, device)
            for q in range(groups):
                tbl[q] = tbl[q] + clip * gap[it, q]
            for d in range(1, rb):
                p, device = type_peer(d)
                arrive(means.at[it], mean_s.at[it], p, device)

    for it in range(ITERS):
        pltpu.make_async_copy(squares_in.at[it], squares_in.at[it], sq_s.at[0, it]).wait()
    for copy in pending:
        copy.wait_send()


def local(
    mkt, grp,
    mean_utility, market_share, product_traits, taste_draws, taste_scale, type_weight,
    market_size, product_firm, firm_order, loyalty, firm_share,
):
    n_m, J, K = product_traits.shape
    firms, R = firm_share.shape
    owned = loyalty.shape[0]
    rb = R // LANES
    groups = mkt * grp // rb
    rows = n_m * J
    tiles = rows // LANES
    qr = firms // groups

    f32, bf16 = jnp.float32, jnp.bfloat16
    dma = pltpu.SemaphoreType.DMA
    vmem = pltpu.VMEM
    spec = pl.BlockSpec(memory_space=pltpu.VMEM)
    smem = pl.BlockSpec(memory_space=pltpu.SMEM)
    dims = (mkt, grp, rb, groups, n_m, J, K, firms, owned, R)
    scratch = [
        vmem((rb, n_m * K, LANES), f32),
        vmem((rb, n_m, LANES), f32),
        vmem((rb, K + 2, tiles, LANES), f32),
        vmem((rb, owned, LANES), f32),
        vmem((ITERS - 1, rb, tiles, LANES), f32),
        vmem((groups, qr, LANES), f32),
        vmem((qr, LANES), f32),
        vmem((groups, 1, LANES), f32),
        vmem((1, LANES), f32),
        vmem((n_m, R), f32),
        vmem((K + 2, tiles, LANES), f32),
        vmem((n_m * K, rows), f32),
        vmem((rb, rows, firms), bf16),
        vmem((rb, firms, rows), bf16),
        vmem((rb, rows, LANES), f32),
        vmem((firms, LANES), f32),
        vmem((firms, LANES), f32),
        vmem((1, firms), f32),
        vmem((firms, LANES), f32),
        vmem((rb, rows, 2 * LANES), bf16),
        vmem((firms, 2 * LANES), bf16),
        vmem((firms // 2, 2 * LANES), f32),
        vmem((ITERS, rb, tiles, LANES), f32),
        vmem((ITERS, rb, tiles, LANES), f32),
        vmem((ITERS, groups, qr, LANES), f32),
        vmem((ITERS, groups, qr, LANES), f32),
        vmem((ITERS - 1, groups, qr, LANES), f32),
        vmem((ITERS, 1, LANES), f32),
        vmem((ITERS, mkt * grp - 1, 1, LANES), f32),
        vmem((rb, owned, LANES), f32),
        vmem((rb, owned, LANES), f32),
        vmem((rb, owned, LANES), f32),
        vmem((rb, owned, LANES), f32),
        dma,
        dma((2, rb)), dma((2, rb)), dma((2, rb)), dma((2, rb)),
        dma((ITERS - 1, 2, rb)),
        dma((2, groups)), dma((2, groups)),
        dma((ITERS, 2, rb)),
        dma((ITERS, 2, groups)),
        dma((ITERS - 1, 2, groups)),
        dma((2, rb)), dma((2, rb)),
        dma((2, ITERS)),
    ]
    return pl.pallas_call(
        functools.partial(kernel, dims),
        out_shape=(
            jax.ShapeDtypeStruct((n_m, J), f32),
            jax.ShapeDtypeStruct((owned, R), f32),
        ),
        in_specs=[smem] * 2 + [spec] * 8 + [pl.BlockSpec(memory_space=pl.ANY)],
        out_specs=(spec, spec),
        scratch_shapes=scratch,
        compiler_params=pltpu.CompilerParams(
            collective_id=0, has_side_effects=True, vmem_limit_bytes=60 * 1024 * 1024
        ),
    )(
        market_size, taste_scale, taste_draws.transpose(1, 0, 2).reshape(n_m * K, R), type_weight,
        product_traits.transpose(2, 0, 1), product_firm, mean_utility, market_share,
        loyalty, firm_order.reshape(firms // LANES, LANES), firm_share,
    )


def solution(mesh):
    both = ("mkt", "grp")
    placed = (
        P(both, None), P(both, None), P(both, None, None), P(both, None, None), P(),
        P(both, None), P(both), P(both, None), P(), P(both, None), P(),
    )
    return jax.shard_map(
        functools.partial(local, mesh.shape["mkt"], mesh.shape["grp"]),
        mesh=mesh,
        in_specs=placed,
        out_specs=(P(both, None), P(both, None)),
        check_vma=False,
    )
```

time: 99.4 us -> 88.1 us (0.89)
  Pallas kernels: 89.2 us -> 84.5 us
  local copies, waits for them, and re-layouts: 6.43 us -> 2.77 us
  other arithmetic: 2.67 us -> 0 us
    pallas_call x1, Pallas kernels: 89.2 us -> 84.5 us  [local(): pl.pallas_call(functools.partial(kernel, dims), out_shape=(jax.ShapeDtype...]
    reshape x8 -> x0, local copies, waits for them, and re-layouts: 3.67 us -> none  [the longest x1 1.34 us: local(): return (mean_new.reshape(n_m, J), loyalty_new)]
    concatenate x2 -> x0, other arithmetic: 1.46 us -> none  [the longest x1 0.77 us: local(): wide_own = jnp.concatenate([taste_draws.reshape(n_m * K, R), mass], axis=0)]
    reduce_sum x1 -> x0, other arithmetic: 1.07 us -> none  [local(): base = jnp.log(market_share) + jnp.log(jnp.sum(mass, axis=1))[:, None]]
    unnamed x14 -> x2, local copies, waits for them, and re-layouts: 2.68 us -> 2.77 us
where the time goes in v2:
time: 88.1 us; the launch traced here: 87.9 us
  Pallas kernels  84.5 us (96%)
  local copies, waits for them, and re-layouts  2.77 us (3%)
    pallas_call x1, Pallas kernels, local(): pl.pallas_call(functools.partial(kernel, dims), out_shape=(jax.ShapeDtype...  84.5 us
    unnamed x2, local copies, waits for them, and re-layouts  2.77 us

profile of v2, /device:TPU:0, one launch (start us, length us, event | category | flops | bytes accessed | tf_op | source)
XLA Modules:
  0.0 87.9 jit_solution(10694471133246648394)
XLA Ops:
  0.6 84.5 %shard_map.122 = (f32[16,64]{1,0:T(8,128)}, f32[16,1024]{1,0:T(8,128)}) custom-call(f32[16]{0:T(128)} %size_ref.1, f32[5]{0:T(128)} %scale_ref.1, f32[80,1024]{1,0:T(8,128)} %bitcast.5, f32[16,1024]{1,0:T(8,128)} %weight_ref.1, f32[5,16,64]{2,1,0:T(8,128)} %bitcast.6, s32[16,64]{1,0:T(8,128)} %firm_ref.1, f32[16,64]{1,0:T(8,128)} %mean_ref.1, ...), custom_call_target="tpu_custom_call" | custom-call | tf_op jit(solution)/shard_map/pallas_call | solution.py:430
  85.1 1.3 %copy.15 = f32[16,64]{1,0:T(8,128)} copy(f32[16,64]{1,0:T(8,128)} %get-tuple-element.4) | data formatting | bytes 8192
  86.4 1.5 %copy.16 = f32[16,1024]{1,0:T(8,128)} copy(f32[16,1024]{1,0:T(8,128)} %get-tuple-element.5) | data formatting | bytes 131072
